TPU v7x, 32 devices: a whole 2x2x4 slice. The times are simulated.
32 devices in a mesh: dp: 2 (over core), wide: 4 (over y, x), narrow: 4 (over z).
Axes of the slice: x: 2, y: 2, z: 4, core: 2. Of those that a mesh axis runs over, the one named last changes fastest.
Arguments:
- block_input: float32 [1600, 4096], P('wide', ('dp', 'narrow')), as said below
- block_cotangent: float32 [1600, 4096], P('wide', ('dp', 'narrow')), may hold values from -6 to 6
- seq_start: int32 [32, 128], P(('dp', 'wide', 'narrow')), may hold values from 0 to 127, as said below
- ln1_gain: float32 [1600], P('wide'), may hold values from 0.5 to 1.5
- ln1_shift: float32 [1600], P('wide'), may hold values from -2 to 2
- w_qkv: float32 [1600, 3, 1600], P('wide', None, 'narrow'), may hold values from -0.15625 to 0.15625
- b_qv: float32 [2, 1600], P(None, 'narrow'), may hold values from -3 to 3
- w_out: float32 [1600, 1600], P('wide', 'narrow'), may hold values from -0.4375 to 0.4375
- b_out: float32 [1600], P('wide'), may hold values from -2 to 2
- ln2_gain: float32 [1600], P('wide'), may hold values from 0.5 to 1.5
- ln2_shift: float32 [1600], P('wide'), may hold values from -2 to 2
- w_fc: float32 [1600, 6400], P('wide', 'narrow'), may hold values from -0.15625 to 0.15625
- b_fc: float32 [6400], P('narrow'), may hold values from -3 to 3
- w_proj: float32 [1600, 6400], P('wide', 'narrow'), may hold values from -0.078125 to 0.078125
- b_proj: float32 [1600], P('wide'), may hold values from -2 to 2
Outputs:
- block_output: float32 [1600, 4096], P('wide', ('dp', 'narrow'))
- input_grad: float32 [1600, 4096], P('wide', ('dp', 'narrow'))
- grad_ln1_gain: float32 [1600], P('wide')
- grad_ln1_shift: float32 [1600], P('wide')
- grad_w_qkv: float32 [1600, 3, 1600], P('wide', None, 'narrow')
- grad_b_qv: float32 [2, 1600], P(None, 'narrow')
- grad_w_out: float32 [1600, 1600], P('wide', 'narrow')
- grad_b_out: float32 [1600], P('wide')
- grad_ln2_gain: float32 [1600], P('wide')
- grad_ln2_shift: float32 [1600], P('wide')
- grad_w_fc: float32 [1600, 6400], P('wide', 'narrow')
- grad_b_fc: float32 [6400], P('narrow')
- grad_w_proj: float32 [1600, 6400], P('wide', 'narrow')
- grad_b_proj: float32 [1600], P('wide')
Inputs may be any that keep to these rules, and one draw needn't show every extreme that they name: `block_input`: token activations of order one, with scales that differ from token to token. `seq_start`: along each row the values never fall; each equals the token's own position at the first token of its sequence and the start of its sequence after it. Block 0 holds one sequence of 128 tokens; some block ends with a sequence of one token.
All inputs are finite; a program needn't handle non-finite values.
Results may differ from a plain program's by a relative error of at most 0.011.
Values may be sent and summed in bfloat16 or wider, within the bound.
A program may use at most 320 MiB of HBM per device.

v0:
```python
import math
import jax
import jax.numpy as jnp
from jax import lax
from jax.sharding import PartitionSpec as P

HEADS = 25
HEAD = 64
EPS = 1e-05
GELU_C = math.sqrt(2.0 / math.pi)
BF = jnp.bfloat16
F32 = jnp.float32


def gelu_value(pre_act):
    inner = GELU_C * (pre_act + 0.044715 * pre_act * pre_act * pre_act)
    return 0.5 * pre_act * (1.0 + jnp.tanh(inner))


def gelu_slope(pre_act):
    tanh_part = jnp.tanh(GELU_C * (pre_act + 0.044715 * pre_act * pre_act * pre_act))
    return 0.5 * (1.0 + tanh_part) + 0.5 * pre_act * (1.0 - tanh_part * tanh_part) * GELU_C * (
        1.0 + 3.0 * 0.044715 * pre_act * pre_act
    )


def dot(a, b, ca, cb):
    return lax.dot_general(a, b, (((ca,), (cb,)), ((), ())), preferred_element_type=F32)


def row_totals(first_term, second_term):
    return lax.psum(
        (jnp.sum(first_term, axis=1, keepdims=True), jnp.sum(second_term, axis=1, keepdims=True)),
        "wide",
    )


def norm_forward(inputs, gain_shard, shift_shard):
    full_width = inputs.shape[1] * lax.axis_size("wide")
    total_sum, square_sum = row_totals(inputs, inputs * inputs)
    mean_row = total_sum / full_width
    inv_std = lax.rsqrt(square_sum / full_width - mean_row * mean_row + EPS)
    normed = (inputs - mean_row) * inv_std
    return (normed, inv_std, (normed * gain_shard + shift_shard).astype(BF))


def norm_backward(row_grads, normed, inv_std, gain_shard):
    full_width = row_grads.shape[1] * lax.axis_size("wide")
    scaled = row_grads * gain_shard
    first_sum, second_sum = row_totals(scaled, scaled * normed)
    return inv_std * (scaled - first_sum / full_width - normed * (second_sum / full_width))


def gather_tokens(values):
    return lax.all_gather(values, "wide", axis=0, tiled=True)


def gather_narrow(values):
    return lax.all_gather(values, "narrow", axis=0, tiled=True)


def sum_tokens(partial_value):
    return lax.psum_scatter(
        partial_value.astype(BF), "wide", scatter_dimension=0, tiled=True
    ).astype(F32)


def sum_narrow(partial_value):
    return lax.psum_scatter(
        partial_value.astype(BF), "narrow", scatter_dimension=0, tiled=True
    ).astype(F32)


def to_tokens(values):
    return lax.all_to_all(values, "wide", split_axis=0, concat_axis=1, tiled=True)


def to_features(values):
    return lax.all_to_all(values, "wide", split_axis=1, concat_axis=0, tiled=True)


def block_mask(starts):
    position = jnp.arange(starts.shape[0])
    return (position[None, :] <= position[:, None]) & (starts[:, None] == starts[None, :])


def split_heads(values):
    return values.reshape(values.shape[0], HEADS, HEAD)


def attend_forward(heads_all, allowed):
    score_scale = 1.0 / math.sqrt(HEAD)
    queries = split_heads(heads_all[:, 0])
    keys_part = split_heads(heads_all[:, 1])
    values_part = split_heads(heads_all[:, 2])
    scores = (
        jnp.einsum("ihd,jhd->hij", queries, keys_part, preferred_element_type=F32) * score_scale
    )
    log_total = jnp.log(jnp.sum(jnp.where(allowed, jnp.exp(scores), 0.0), axis=2, keepdims=True))
    attn_probs = jnp.where(allowed, jnp.exp(scores - log_total), 0.0).astype(BF)
    attended = jnp.einsum("hij,jhd->ihd", attn_probs, values_part, preferred_element_type=F32)
    return (attended.reshape(heads_all.shape[0], HEADS * HEAD).astype(BF), log_total)


def attend_backward(heads_all, allowed, log_total, attended_cot):
    score_scale = 1.0 / math.sqrt(HEAD)
    queries = split_heads(heads_all[:, 0])
    keys_part = split_heads(heads_all[:, 1])
    values_part = split_heads(heads_all[:, 2])
    scores = (
        jnp.einsum("ihd,jhd->hij", queries, keys_part, preferred_element_type=F32) * score_scale
    )
    probs_full = jnp.where(allowed, jnp.exp(scores - log_total), 0.0)
    cot_heads = split_heads(attended_cot)
    dprobs = jnp.einsum("ihd,jhd->hij", cot_heads, values_part, preferred_element_type=F32)
    row_delta = jnp.sum(probs_full * dprobs, axis=2, keepdims=True)
    score_cot = (probs_full * (dprobs - row_delta) * score_scale).astype(BF)
    query_grad = jnp.einsum("hij,jhd->ihd", score_cot, keys_part, preferred_element_type=F32)
    key_grad = jnp.einsum("hij,ihd->jhd", score_cot, queries, preferred_element_type=F32)
    value_grad = jnp.einsum(
        "hij,ihd->jhd", probs_full.astype(BF), cot_heads, preferred_element_type=F32
    )
    stacked = jnp.stack([query_grad, key_grad, value_grad], axis=1)
    return stacked.reshape(heads_all.shape[0], 3, HEADS * HEAD)


def own_half(values, axis):
    half = values.shape[axis] // lax.axis_size("dp")
    return lax.dynamic_slice_in_dim(values, lax.axis_index("dp") * half, half, axis)


def local(
    block_input,
    block_cotangent,
    seq_start,
    ln1_gain,
    ln1_shift,
    w_qkv,
    b_qv,
    w_out,
    b_out,
    ln2_gain,
    ln2_shift,
    w_fc,
    b_fc,
    w_proj,
    b_proj,
):
    cores, wide, narrow = (lax.axis_size("dp"), lax.axis_size("wide"), lax.axis_size("narrow"))
    w_index, n_index = (lax.axis_index("wide"), lax.axis_index("narrow"))
    feats, part = (w_qkv.shape[0], w_qkv.shape[2])
    width = feats * wide
    hid = w_fc.shape[1]
    perm = []
    for w in range(wide):
        for n in range(narrow):
            block = n * wide + w
            perm.append((block, w * narrow + n))
    starts = lax.ppermute(seq_start, ("wide", "narrow"), perm)[0]
    allowed = block_mask(starts)
    wq_mine = own_half(w_qkv.astype(BF).reshape(feats, 3 * part), 0)
    wq_all = lax.all_gather(wq_mine, ("narrow", "dp"), axis=0, tiled=True)
    wq_all = wq_all.reshape(narrow, feats, 3 * part)
    wo_mine = lax.all_gather(own_half(w_out.astype(BF), 0), "narrow", axis=1, tiled=True)
    wo_all = lax.all_gather(wo_mine, ("wide", "dp"), axis=0, tiled=True)
    wf_all = lax.all_gather(own_half(w_fc.astype(BF), 0), ("wide", "dp"), axis=0, tiled=True)
    wp_all = lax.all_gather(own_half(w_proj.astype(BF), 0), ("wide", "dp"), axis=0, tiled=True)
    b_out_full, gain_two_full, shift_two_full = lax.all_gather(
        jnp.stack([b_out, ln2_gain, ln2_shift]), "wide", axis=1, tiled=True
    )
    bias_qv = lax.all_gather(b_qv, "narrow", axis=0).reshape(narrow, 1, 2, part)
    bias_three = jnp.concatenate(
        [bias_qv[:, :, 0], jnp.zeros((narrow, 1, part), F32), bias_qv[:, :, 1]], axis=2
    )
    rows_input = block_input.T
    rows_cot = block_cotangent.T
    x_tok = to_tokens(rows_input)
    dy_tok = to_tokens(rows_cot)
    cot_all = gather_narrow(dy_tok.astype(BF))
    normed_one, inv_one, norm_one = norm_forward(rows_input, ln1_gain, ln1_shift)
    qkv_part = jnp.einsum("tk,nkc->tnc", norm_one, wq_all, preferred_element_type=F32)
    qkv_rows = sum_tokens(qkv_part.transpose(0, 1, 2)).transpose(1, 0, 2)
    qkv_rows = (qkv_rows + bias_three).astype(BF)
    heads_all = qkv_rows.reshape(narrow, -1, 3, part).transpose(1, 2, 0, 3).reshape(-1, 3, width)
    attended, log_total = attend_forward(heads_all, allowed)
    residual = x_tok + dot(attended, wo_all, 1, 1) + b_out_full
    mean_two = jnp.mean(residual, axis=1, keepdims=True)
    inv_two = lax.rsqrt(
        jnp.mean(residual * residual, axis=1, keepdims=True) - mean_two * mean_two + EPS
    )
    normed_two = (residual - mean_two) * inv_two
    norm_two = (normed_two * gain_two_full + shift_two_full).astype(BF)
    norm_two_all = gather_narrow(norm_two)
    pre_act = dot(norm_two_all, wf_all, 1, 0) + b_fc
    hidden = gelu_value(pre_act).astype(BF)
    out_tok = residual + sum_narrow(dot(hidden, wp_all, 1, 1))
    output_rows = to_features(out_tok) + b_proj
    pre_grad = dot(cot_all, wp_all, 1, 0) * gelu_slope(pre_act)
    pre_cot = pre_grad.astype(BF)
    norm_two_grad = sum_narrow(dot(pre_cot, wf_all, 1, 1))

    def reduce_wide(grad):
        total = lax.psum_scatter(grad.astype(BF), ("wide", "dp"), scatter_dimension=0, tiled=True)
        return total

    def share(total):
        return lax.all_gather(total, "dp", axis=0, tiled=True).astype(F32)

    grad_w_proj = share(reduce_wide(dot(cot_all, hidden, 0, 0)))
    grad_w_fc = share(reduce_wide(dot(norm_two_all, pre_cot, 0, 0)))
    scaled = norm_two_grad * gain_two_full
    mean_scaled = jnp.mean(scaled, axis=1, keepdims=True)
    mean_cross = jnp.mean(scaled * normed_two, axis=1, keepdims=True)
    resid_grad = dy_tok + inv_two * (scaled - mean_scaled - normed_two * mean_cross)
    resid_cot = resid_grad.astype(BF)
    attended_cot = dot(resid_cot, wo_all, 1, 0).astype(BF)
    wo_grad = reduce_wide(dot(resid_cot, attended, 0, 0))
    wo_grad = lax.psum_scatter(wo_grad, "narrow", scatter_dimension=1, tiled=True)
    grad_w_out = share(wo_grad)
    qkv_grad = attend_backward(heads_all, allowed, log_total, attended_cot)
    qkv_cot = qkv_grad.astype(BF).reshape(-1, 3, narrow, part).transpose(0, 2, 1, 3)
    qkv_cot_all = gather_tokens(qkv_cot.reshape(-1, narrow, 3 * part))
    norm_one_grad = jnp.einsum("tnc,nkc->tk", qkv_cot_all, wq_all, preferred_element_type=F32)
    wq_grad = jnp.einsum("tk,tnc->nkc", norm_one, qkv_cot_all, preferred_element_type=F32).astype(
        BF
    )
    wq_grad = lax.psum_scatter(
        wq_grad.reshape(narrow * feats, 3 * part), ("narrow", "dp"), scatter_dimension=0, tiled=True
    )
    grad_w_qkv = share(wq_grad).reshape(feats, 3, part)
    resid_back = to_features(resid_grad)
    grad_input_rows = resid_back + norm_backward(norm_one_grad, normed_one, inv_one, ln1_gain)
    qkv_sums = jnp.sum(qkv_grad, axis=0)
    fc_full = lax.dynamic_update_slice_in_dim(
        jnp.zeros((narrow * hid,), F32), jnp.sum(pre_grad, axis=0), n_index * hid, 0
    )
    token_terms = jnp.stack(
        [
            qkv_sums[0],
            qkv_sums[2],
            jnp.sum(resid_grad, axis=0),
            jnp.sum(norm_two_grad * normed_two, axis=0),
            jnp.sum(norm_two_grad, axis=0),
        ]
    )
    feature_terms = jnp.stack(
        [
            jnp.sum(norm_one_grad * normed_one, axis=0),
            jnp.sum(norm_one_grad, axis=0),
            jnp.sum(rows_cot, axis=0),
        ]
    )
    feature_full = lax.dynamic_update_slice_in_dim(
        jnp.zeros((3, width), F32), feature_terms, w_index * feats, 1
    )
    token_sum, feature_sum, fc_sum = lax.psum(
        (token_terms, feature_full, fc_full), ("dp", "wide", "narrow")
    )
    grad_b_qv = lax.dynamic_slice_in_dim(token_sum[:2], n_index * part, part, 1)
    out_bias, gain_two, shift_two = lax.dynamic_slice_in_dim(
        token_sum[2:], w_index * feats, feats, 1
    )
    gain_one, shift_one, proj_bias = lax.dynamic_slice_in_dim(
        feature_sum, w_index * feats, feats, 1
    )
    grad_b_fc = lax.dynamic_slice_in_dim(fc_sum, n_index * hid, hid, 0)
    return (
        output_rows.T,
        grad_input_rows.T,
        gain_one,
        shift_one,
        grad_w_qkv,
        grad_b_qv,
        grad_w_out,
        out_bias,
        gain_two,
        shift_two,
        grad_w_fc,
        grad_b_fc,
        grad_w_proj,
        proj_bias,
    )


def solution(mesh):
    return jax.shard_map(
        local,
        mesh=mesh,
        in_specs=(
            P("wide", ("dp", "narrow")),
            P("wide", ("dp", "narrow")),
            P(("dp", "wide", "narrow"), None),
            P("wide"),
            P("wide"),
            P("wide", None, "narrow"),
            P(None, "narrow"),
            P("wide", "narrow"),
            P("wide"),
            P("wide"),
            P("wide"),
            P("wide", "narrow"),
            P("narrow"),
            P("wide", "narrow"),
            P("wide"),
        ),
        out_specs=(
            P("wide", ("dp", "narrow")),
            P("wide", ("dp", "narrow")),
            P("wide"),
            P("wide"),
            P("wide", None, "narrow"),
            P(None, "narrow"),
            P("wide", "narrow"),
            P("wide"),
            P("wide"),
            P("wide"),
            P("wide", "narrow"),
            P("narrow"),
            P("wide", "narrow"),
            P("wide"),
        ),
        check_vma=False,
    )
```

profile of v0, /device:TPU:9, one launch (start us, length us, event | category | flops | bytes accessed | tf_op | source)
XLA Modules:
  0.0 814.7 jit_solution(4616256458298618883)
XLA Ops:
  18.2 7.9 all-reduce.5
  26.2 38.4 %all-gather.13.cloned.1.call-done = bf16[1600,1200]{1,0:T(8,128)(2,1)} async-done(((bf16[200,1200]{1,0:T(8,128)(2,1)}), bf16[1600,1200]{1,0:T(8,128)(2,1)}) %all-gather.13.cloned.1.call-update) | async-done | bytes 3840016 | tf_op jit(solution)/shard_map/all_gather | solution.py:162
  64.6 8.2 %convolution_convert_fusion.3 = bf16[512,4,1200]{0,2,1:T(8,128)(2,1)} fusion(bf16[4,400,1200]{2,1,0:T(8,128)(2,1)} %bitcast.247, f32[400,512]{1,0:T(8,128)S(1)} %copy-done.2, f32[400]{0:T(512)S(1)} %copy-done.25, f32[400]{0:T(512)S(1)} %copy-done.23, f32[512]{0:T(512)S(1)} %bitcast.228, f32[512]{0:T(512)S(1)} %bitcast.224), kind=kOutput, calls=%fused_computation.6 | convolution fusion | flops 1969561600 | bytes 9581696 | tf_op jit(solution)/shard_map/tk,nkc->tnc/dot_general | solution.py:181
  72.8 7.5 copy.132
  83.8 17.2 %all_gather.48 = bf16[200,1600]{0,1:T(8,128)(2,1)} all-gather(bf16[200,400]{0,1:T(8,128)(2,1)} %copy.136), channel_id=1, replica_groups=mesh['dp'=2,'wide'=4,'narrow'=4] {'narrow'}, dimensions={1}, use_global_device_ids=true | all-gather | bytes 800000 | tf_op jit(solution)/shard_map/all_gather | solution.py:164
  113.9 22.5 %all-gather.2 = f32[4,400,3]{1,2,0:T(4,128)S(1)} all-gather(f32[1,400,3]{1,2,0:T(4,128)S(1)} %maximum_bitcast_fusion.1), channel_id=1, replica_groups=mesh['dp'=2,'wide'=4,'narrow'=4] {'wide'}, dimensions={0}, use_global_device_ids=true | all-gather | bytes 24000 | tf_op jit(solution)/shard_map/all_gather | solution.py:168
  136.5 11.8 %all-gather.1 = f32[4,2,400]{2,1,0:T(2,128)S(1)} all-gather(f32[1,2,400]{2,1,0:T(2,128)S(1)} %bitcast.232), channel_id=2, replica_groups=mesh['dp'=2,'wide'=4,'narrow'=4] {'narrow'}, dimensions={0}, use_global_device_ids=true | all-gather | bytes 16000 | tf_op jit(solution)/shard_map/all_gather | solution.py:171
  167.7 18.7 %all_to_all.76 = f32[4,128,400]{1,2,0:T(8,128)S(1)} all-to-all(f32[4,128,400]{1,2,0:T(8,128)S(1)} %copy_bitcast_fusion), channel_id=1, replica_groups=mesh['dp'=2,'wide'=4,'narrow'=4] {'wide'}, dimensions={0} | all-to-all | bytes 1638400 | tf_op jit(solution)/shard_map/all_to_all | solution.py:75
  189.8 22.8 %all-gather.19.cloned.1.call-done = bf16[1600,1600]{1,0:T(8,128)(2,1)} async-done(((bf16[200,1600]{1,0:T(8,128)(2,1)}), bf16[1600,1600]{1,0:T(8,128)(2,1)}) %all-gather.19.cloned.1.call-update) | async-done | bytes 5120016 | tf_op jit(solution)/shard_map/all_gather | solution.py:166
  212.7 37.3 %all-gather.17.cloned.1.call-done = bf16[512,1600]{0,1:T(8,128)(2,1)} async-done(((bf16[128,1600]{0,1:T(8,128)(2,1)}), bf16[512,1600]{0,1:T(8,128)(2,1)}) %all-gather.17.cloned.1.call-update) | async-done | bytes 1638416 | tf_op jit(solution)/shard_map/all_gather | solution.py:59
  250.0 7.9 convolution_add_fusion
  257.9 31.1 %all-gather.23.cloned.1.call-done = bf16[512,1600]{0,1:T(8,128)(2,1)} async-done(((bf16[128,1600]{0,1:T(8,128)(2,1)}), bf16[512,1600]{0,1:T(8,128)(2,1)}) %all-gather.23.cloned.1.call-update) | async-done | bytes 1638416 | tf_op jit(solution)/shard_map/all_gather | solution.py:59
  289.0 45.2 %all-gather.21.cloned.1.call-done = bf16[1600,1600]{1,0:T(8,128)(2,1)} async-done(((bf16[200,1600]{1,0:T(8,128)(2,1)}), bf16[1600,1600]{1,0:T(8,128)(2,1)}) %all-gather.21.cloned.1.call-update) | async-done | bytes 5120016 | tf_op jit(solution)/shard_map/all_gather | solution.py:167
  334.3 9.2 %fusion.89 = (f32[1600]{0:T(1024)S(1)}, bf16[512,1600]{0,1:T(8,128)(2,1)S(1)}) fusion(f32[512,1600]{0,1:T(8,128)} %convolution_add_fusion, bf16[1600,1600]{1,0:T(8,128)(2,1)} %all-gather.21.cloned.1.call-done, bf16[512,1600]{0,1:T(8,128)(2,1)} %all-gather.23.cloned.1.call-done), kind=kOutput, calls=%fused_computation.128 | convolution fusion | flops 2637822464 | bytes 11680000 | tf_op jit(solution)/shard_map/dot_general | solution.py:28
  355.2 8.0 convolution_convert_fusion.6
  366.8 8.6 %fusion.2 = bf16[1600,1600]{0,1:T(8,128)(2,1)} fusion(bf16[512,1600]{0,1:T(8,128)(2,1)} %all-gather.23.cloned.1.call-done, f32[512,1600]{0,1:T(8,128)} %convolution_add_fusion), kind=kOutput, calls=%fused_computation.5 | convolution fusion | flops 2631372800 | bytes 10035200 | tf_op jit(solution)/shard_map/dot_general | solution.py:28
  375.5 7.5 convolution_convert_fusion.1
  391.3 37.8 %reduce-scatter.25.cloned.1.call-done = bf16[128,1600]{1,0:T(8,128)(2,1)} async-done(((bf16[512,1600]{1,0:T(8,128)(2,1)}), bf16[128,1600]{1,0:T(8,128)(2,1)}) %reduce-scatter.25.cloned.1.call-update) | async-done | bytes 409616
  463.5 90.7 %all-reduce.9.cloned.1.call-done = bf16[1600,1600]{0,1:T(8,128)(2,1)} async-done(((bf16[1600,1600]{0,1:T(8,128)(2,1)}), bf16[1600,1600]{0,1:T(8,128)(2,1)}) %all-reduce.9.cloned.1.call-update) | async-done | bytes 5120016
  561.0 59.0 %reduce-scatter.35.cloned.1.call-done = bf16[200,1600]{1,0:T(8,128)(2,1)} async-done(((bf16[1600,1600]{1,0:T(8,128)(2,1)}), bf16[200,1600]{1,0:T(8,128)(2,1)}) %reduce-scatter.35.cloned.1.call-update) | async-done | bytes 640016
  628.0 58.3 %reduce-scatter.33.cloned.1.call-done = bf16[200,1600]{1,0:T(8,128)(2,1)} async-done(((bf16[1600,1600]{1,0:T(8,128)(2,1)}), bf16[200,1600]{1,0:T(8,128)(2,1)}) %reduce-scatter.33.cloned.1.call-update) | async-done | bytes 640016
  701.9 7.8 all-to-all-done.1
  717.2 8.4 %all-reduce.4 = (f32[512,1]{0,1:T(1,128)S(1)}, f32[512,1]{0,1:T(1,128)S(1)}) all-reduce(f32[512,1]{0,1:T(1,128)S(1)} %bitcast.245, f32[512,1]{0,1:T(1,128)S(1)} %bitcast.246), channel_id=1, replica_groups=mesh['dp'=2,'wide'=4,'narrow'=4] {'wide'}, use_global_device_ids=true, to_apply=%region_16.17 | all-reduce | flops 1024 | bytes 8192 | tf_op jit(solution)/shard_map/psum | solution.py:32
  726.8 61.2 %all-reduce.11.cloned.1.call-done = (f32[3,1600]{1,0:T(4,128)}, f32[5,1600]{1,0:T(8,128)}, f32[6400]{0:T(1024)}) async-done(((f32[3,1600]{1,0:T(4,128)}, f32[5,1600]{1,0:T(8,128)}, f32[6400]{0:T(1024)}), (f32[3,1600]{1,0:T(4,128)}, f32[5,1600]{1,0:T(8,128)}, f32[6400]{0:T(1024)})) %all-reduce.11.cloned.1.call-update) | async-done | bytes 76816 | tf_op jit(solution)/shard_map/psum | solution.py:256
  (196 shorter events, 164.2 us)
Async XLA Ops:
  8.0 95.4 %copy-start = (f32[400,1600]{1,0:T(8,128)S(1)}, f32[400,1600]{1,0:T(8,128)}, u32[]{:S(2)}) copy-start(f32[400,1600]{1,0:T(8,128)} %param.26) | copy-start | bytes 7680004
  8.0 56.6 %all-gather.13.cloned.1.call-start = ((), (), s32[]{:S(2)}) async-start(), calls=%async_computation.11 | async-start | bytes 4608000 | tf_op jit(solution)/shard_map/all_gather | solution.py:162
  18.0 130.7 %reduce-scatter.23.cloned.1.call-start = ((), (), s32[]{:S(2)}) async-start(), calls=%async_computation.20 | async-start | bytes 6225920
  80.3 81.7 %all-gather.15.cloned.1.call-start = ((), (), s32[]{:S(2)}) async-start(), calls=%async_computation.12 | async-start | bytes 5990400 | tf_op jit(solution)/shard_map/all_gather | solution.py:165
  103.3 109.3 %all-gather.19.cloned.1.call-start = ((), (), s32[]{:S(2)}) async-start(), calls=%async_computation.14 | async-start | bytes 5990400 | tf_op jit(solution)/shard_map/all_gather | solution.py:166
  104.4 44.2 %collective-permute-start = (s32[1,128]{1,0:T(1,128)S(1)}, s32[1,128]{1,0:T(1,128)S(1)}, u32[]{:S(2)}, u32[]{:S(2)}) collective-permute-start(s32[1,128]{1,0:T(1,128)S(1)} %copy-done.26), channel_id=1, source_target_pairs={{0,0},{4,1},{8,2},{12,3},{1,4},{5,5},{9,6},{13,7},{2,8},{6,9},{10,... | collective-permute-start | bytes 1544 | tf_op jit(solution)/shard_map/ppermute | solution.py:159
  109.6 46.8 %all-to-all-start = ((f32[4,128,400]{1,2,0:T(8,128)}), f32[4,128,400]{1,2,0:T(8,128)}, u32[]{:S(2)}, u32[]{:S(2)}) async-start(f32[4,128,400]{1,2,0:T(8,128)} %copy_bitcast_fusion.1), calls=%async_computation | async-start | bytes 1638400 | tf_op jit(solution)/shard_map/all_to_all | solution.py:75
  113.8 136.2 %all-gather.17.cloned.1.call-start = ((), (), s32[]{:S(2)}) async-start(), calls=%async_computation.13 | async-start | bytes 2048000 | tf_op jit(solution)/shard_map/all_gather | solution.py:59
  167.6 121.4 %all-gather.23.cloned.1.call-start = ((), (), s32[]{:S(2)}) async-start(), calls=%async_computation.16 | async-start | bytes 2048000 | tf_op jit(solution)/shard_map/all_gather | solution.py:59
  187.3 147.0 %all-gather.21.cloned.1.call-start = ((), (), s32[]{:S(2)}) async-start(), calls=%async_computation.15 | async-start | bytes 5990400 | tf_op jit(solution)/shard_map/all_gather | solution.py:167
  189.6 200.4 %reduce-scatter.27.cloned.1.call-start = ((), (), s32[]{:S(2)}) async-start(), calls=%async_computation.22 | async-start | bytes 2129920
  355.0 74.1 %reduce-scatter.25.cloned.1.call-start = ((), (), s32[]{:S(2)}) async-start(), calls=%async_computation.21 | async-start | bytes 2129920
  366.8 187.4 %all-reduce.9.cloned.1.call-start = ((), (), s32[]{:S(2)}) async-start(), calls=%async_computation.25 | async-start | bytes 10649600
  375.5 244.5 %reduce-scatter.35.cloned.1.call-start = ((), (), s32[]{:S(2)}) async-start(), calls=%async_computation.27 | async-start | bytes 5990400
  383.1 237.9 %all-gather.25.cloned.1.call-start = ((), (), s32[]{:S(2)}) async-start(), calls=%async_computation.17 | async-start | bytes 6144000 | tf_op jit(solution)/shard_map/all_gather | solution.py:55
  456.5 229.8 %reduce-scatter.33.cloned.1.call-start = ((), (), s32[]{:S(2)}) async-start(), calls=%async_computation.26 | async-start | bytes 5990400
  461.6 237.3 %all-gather.29.cloned.1.call-start = ((), (), s32[]{:S(2)}) async-start(), calls=%async_computation.19 | async-start | bytes 1996800 | tf_op jit(solution)/shard_map/all_gather | solution.py:207
  463.5 93.6 %copy-start.4 = (f32[400,512]{1,0:T(8,128)S(1)}, f32[400,512]{1,0:T(8,128)}, u32[]{:S(2)}) copy-start(f32[400,512]{1,0:T(8,128)} %param.16) | copy-start | bytes 2457604
  557.0 157.3 %all-gather.27.cloned.1.call-start = ((), (), s32[]{:S(2)}) async-start(), calls=%async_computation.18 | async-start | bytes 1996800 | tf_op jit(solution)/shard_map/all_gather | solution.py:207
  620.0 168.0 %all-reduce.11.cloned.1.call-start = ((), (), s32[]{:S(2)}) async-start(), calls=%async_computation.28 | async-start | bytes 217088 | tf_op jit(solution)/shard_map/psum | solution.py:256
  628.0 165.9 %reduce-scatter.31.cloned.1.call-start = ((), (), s32[]{:S(2)}) async-start(), calls=%async_computation.24 | async-start | bytes 1024000
  688.6 111.3 %reduce-scatter.29.cloned.1.call-start = ((), (), s32[]{:S(2)}) async-start(), calls=%async_computation.23 | async-start | bytes 4608000 | tf_op jit(solution)/shard_map/reduce_scatter | solution.py:227
  695.3 14.4 %all-to-all-start.1 = ((f32[128,4,400]{0,2,1:T(8,128)}), f32[128,4,400]{0,2,1:T(8,128)S(1)}, u32[]{:S(2)}, u32[]{:S(2)}) async-start(f32[128,4,400]{0,2,1:T(8,128)} %bitcast.30), calls=%async_computation.1 | async-start | bytes 1638400 | tf_op jit(solution)/shard_map/all_to_all | solution.py:79
  709.7 16.0 %all-to-all-start.3 = ((f32[128,4,400]{0,2,1:T(8,128)}), f32[128,4,400]{0,2,1:T(8,128)S(1)}, u32[]{:S(2)}, u32[]{:S(2)}) async-start(f32[128,4,400]{0,2,1:T(8,128)} %bitcast.38), calls=%async_computation.3 | async-start | bytes 1638400 | tf_op jit(solution)/shard_map/all_to_all | solution.py:79
  (27 other events, 343.6 us)
Sparse Core Ops, SparseCore 0:
  18.1 46.4 all-gather.12
  80.5 66.6 reduce-scatter.22
  456.6 59.4 all-gather.24
  557.1 10.3 all-gather.28
  620.1 10.3 all-gather.26
  636.4 151.6 all-reduce.10
Sparse Core Ops, SparseCore 1:
  103.4 58.6 all-gather.14
  164.3 48.3 all-gather.18
  214.7 35.3 all-gather.16
  252.2 36.8 all-gather.22
  291.5 42.7 all-gather.20
  355.1 34.9 reduce-scatter.26
  392.8 36.3 reduce-scatter.24
  432.3 121.8 all-reduce.8
  557.4 62.5 reduce-scatter.34
  623.4 62.8 reduce-scatter.32
  689.0 21.4 reduce-scatter.30
  712.9 50.0 reduce-scatter.28
where the time goes:
time: 824 us; the launch traced here: 815 us
  waiting for transfers between devices  499 us (61%)
  matrix products  105 us (13%)
  blocking collectives  93.2 us (11%)
  local copies, waits for them, and re-layouts  59.8 us (7%)
  other arithmetic  23.3 us (3%)
  starting transfers between devices  17.2 us (2%)
  between operations  17.2 us (2%)
    unnamed x25, waiting for transfers between devices  250 us
    all_gather x2, waiting for transfers between devices, gather_narrow(): return lax.all_gather(values, 'narrow', axis=0, tiled=True)  68.5 us
    dot_general x9, matrix products, dot(): lax.dot_general(a, b, (((ca,), (cb,)), ((), ())), preferred_element_type=...  62.2 us
    psum x1, waiting for transfers between devices, local(): lax.psum((token_terms, feature_full, fc_full), ('dp', 'wide', 'narrow'))  61.2 us
    all_gather x1, waiting for transfers between devices, local(): lax.all_gather(own_half(w_proj.astype(BF), 0), ('wide', 'dp'), axis=0, ti...  45.2 us
    all_gather x1, waiting for transfers between devices, local(): wq_all = lax.all_gather(wq_mine, ('narrow', 'dp'), axis=0, tiled=True)  38.4 us
    unnamed x72, local copies, waits for them, and re-layouts  33.5 us
    all_gather x1, waiting for transfers between devices, local(): lax.all_gather(own_half(w_fc.astype(BF), 0), ('wide', 'dp'), axis=0, tile...  22.8 us
  transfers between devices with their start and end apart: 22, of which 13 were waited for; matrix products, arithmetic and copies ran while one was open for 17% of the time, Pallas kernels for 0%

commit v1 on v0

--- a/solution.py
+++ b/solution.py
@@ -10,6 +10,28 @@
 GELU_C = math.sqrt(2.0 / math.pi)
 BF = jnp.bfloat16
 F32 = jnp.float32
+
+
+def joined_along(parts, dim):
+    parts = jnp.moveaxis(parts, 0, dim)
+    shape = parts.shape
+    return parts.reshape(*shape[:dim], shape[dim] * shape[dim + 1], *shape[dim + 2 :])
+
+
+def doubled(x, axis):
+    peers = lax.axis_size(axis)
+    pieces = x[None]
+    for level in range(peers.bit_length() - 1):
+        bit = 1 << level
+        partner_block = lax.ppermute(pieces, axis, [(i, i ^ bit) for i in range(peers)])
+        both = jnp.stack([pieces, partner_block])
+        upper = lax.axis_index(axis) >> level & 1
+        pieces = jnp.where(upper == 0, both, both[::-1]).reshape(-1, *x.shape)
+    return pieces
+
+
+def gather_by_bits(array, axis, dim):
+    return joined_along(doubled(array, axis), dim)
 
 
 def gelu_value(pre_act):
@@ -56,7 +78,7 @@
 
 
 def gather_narrow(values):
-    return lax.all_gather(values, "narrow", axis=0, tiled=True)
+    return gather_by_bits(values, "narrow", 0)
 
 
 def sum_tokens(partial_value):

time: 824 us -> 733 us (0.89)
  waiting for transfers between devices: 499 us -> 407 us
  blocking collectives: 93.2 us -> 73.4 us
  starting transfers between devices: 17.2 us -> 27.1 us
    all_gather x2 -> x0, waiting for transfers between devices: 68.5 us -> none  [gather_narrow(): return lax.all_gather(values, 'narrow', axis=0, tiled=True)]
    all_gather x1, waiting for transfers between devices: 0.01 us -> 59.9 us  [gather_tokens(): return lax.all_gather(values, 'wide', axis=0, tiled=True)]
    unnamed x25 -> x23, waiting for transfers between devices: 250 us -> 196 us
    ppermute x0 -> x4, waiting for transfers between devices: none -> 50.5 us  [doubled(): lax.ppermute(pieces, axis, [(i, i ^ bit) for i in range(peers)])]
    all_gather x1, waiting for transfers between devices: 45.2 us -> 2.26 us  [local(): lax.all_gather(own_half(w_proj.astype(BF), 0), ('wide', 'dp'), axis=0, ti...]
    all_gather x1, waiting for transfers between devices: 22.8 us -> 0.03 us  [local(): lax.all_gather(own_half(w_fc.astype(BF), 0), ('wide', 'dp'), axis=0, tile...]
    all_to_all x1 -> x0, blocking collectives: 18.7 us -> none  [to_tokens(): lax.all_to_all(values, 'wide', split_axis=0, concat_axis=1, tiled=True)]
    psum x1, waiting for transfers between devices: 61.2 us -> 43.6 us  [local(): lax.psum((token_terms, feature_full, fc_full), ('dp', 'wide', 'narrow'))]
  transfers between devices with their start and end apart: 22 -> 25, of which waited for: 13 -> 14; matrix products, arithmetic and copies ran while one was open for 17% -> 21% of each run, Pallas kernels for 0% -> 0%
where the time goes in v1:
time: 733 us; the launch traced here: 723 us
  waiting for transfers between devices  407 us (56%)
  matrix products  102 us (14%)
  blocking collectives  73.4 us (10%)
  local copies, waits for them, and re-layouts  65.8 us (9%)
  other arithmetic  30.7 us (4%)
  starting transfers between devices  27.1 us (4%)
  between operations  16.7 us (2%)
    unnamed x23, waiting for transfers between devices  196 us
    all_gather x1, waiting for transfers between devices, gather_tokens(): return lax.all_gather(values, 'wide', axis=0, tiled=True)  59.9 us
    dot_general x9, matrix products, dot(): lax.dot_general(a, b, (((ca,), (cb,)), ((), ())), preferred_element_type=...  59.8 us
    ppermute x4, waiting for transfers between devices, doubled(): lax.ppermute(pieces, axis, [(i, i ^ bit) for i in range(peers)])  50.5 us
    psum x1, waiting for transfers between devices, local(): lax.psum((token_terms, feature_full, fc_full), ('dp', 'wide', 'narrow'))  43.6 us
    all_gather x1, waiting for transfers between devices, local(): wq_all = lax.all_gather(wq_mine, ('narrow', 'dp'), axis=0, tiled=True)  38.4 us
    unnamed x74, local copies, waits for them, and re-layouts  31.5 us
    all_gather x1, blocking collectives, local(): lax.all_gather(jnp.stack([b_out, ln2_gain, ln2_shift]), 'wide', axis=1, t...  22.2 us
  transfers between devices with their start and end apart: 25, of which 14 were waited for; matrix products, arithmetic and copies ran while one was open for 21% of the time, Pallas kernels for 0%

profile of v1, /device:TPU:9, one launch (start us, length us, event | category | flops | bytes accessed | tf_op | source)
XLA Modules:
  0.0 723.2 jit_solution(10309658176046283339)
XLA Ops:
  18.2 7.9 %all-reduce.5 = (f32[512,1]{0,1:T(1,128)S(1)}, f32[512,1]{0,1:T(1,128)S(1)}) all-reduce(f32[512,1]{0,1:T(1,128)S(1)} %bitcast.249, f32[512,1]{0,1:T(1,128)S(1)} %bitcast.248), channel_id=1, replica_groups=mesh['dp'=2,'wide'=4,'narrow'=4] {'wide'}, use_global_device_ids=true, to_apply=%region_3.4 | all-reduce | flops 1024 | bytes 8192 | tf_op jit(solution)/shard_map/psum | solution.py:54
  26.2 38.4 %all-gather.11.cloned.1.call-done = bf16[1600,1200]{1,0:T(8,128)(2,1)} async-done(((bf16[200,1200]{1,0:T(8,128)(2,1)}), bf16[1600,1200]{1,0:T(8,128)(2,1)}) %all-gather.11.cloned.1.call-update) | async-done | bytes 3840016 | tf_op jit(solution)/shard_map/all_gather | solution.py:184
  64.6 8.2 %convolution_convert_fusion.3 = bf16[512,4,1200]{0,2,1:T(8,128)(2,1)} fusion(bf16[4,400,1200]{2,1,0:T(8,128)(2,1)} %bitcast.275, f32[400,512]{1,0:T(8,128)S(1)} %copy-done.2, f32[400]{0:T(512)S(1)} %copy-done.28, f32[400]{0:T(512)S(1)} %copy-done.25, f32[512]{0:T(512)S(1)} %bitcast.256, f32[512]{0:T(512)S(1)} %bitcast.252), kind=kOutput, calls=%fused_computation.5 | convolution fusion | flops 1969561600 | bytes 9581696 | tf_op jit(solution)/shard_map/tk,nkc->tnc/dot_general | solution.py:203
  72.8 7.5 %copy.138 = bf16[512,4800]{1,0:T(8,128)(2,1)} copy(bf16[512,4800]{0,1:T(8,128)(2,1)} %bitcast.209) | data formatting | bytes 9830400
  83.9 17.1 %all_gather.42 = bf16[200,1600]{0,1:T(8,128)(2,1)} all-gather(bf16[200,400]{0,1:T(8,128)(2,1)} %copy.142), channel_id=1, replica_groups=mesh['dp'=2,'wide'=4,'narrow'=4] {'narrow'}, dimensions={1}, use_global_device_ids=true | all-gather | bytes 800000 | tf_op jit(solution)/shard_map/all_gather | solution.py:186
  115.6 11.5 %all-gather.1 = f32[4,2,400]{2,1,0:T(2,128)S(1)} all-gather(f32[1,2,400]{2,1,0:T(2,128)S(1)} %bitcast.260), channel_id=2, replica_groups=mesh['dp'=2,'wide'=4,'narrow'=4] {'narrow'}, dimensions={0}, use_global_device_ids=true | all-gather | bytes 16000 | tf_op jit(solution)/shard_map/all_gather | solution.py:193
  135.7 22.2 %all-gather.2 = f32[4,400,3]{1,2,0:T(4,128)S(1)} all-gather(f32[1,400,3]{1,2,0:T(4,128)S(1)} %maximum_bitcast_fusion.1), channel_id=1, replica_groups=mesh['dp'=2,'wide'=4,'narrow'=4] {'wide'}, dimensions={0}, use_global_device_ids=true | all-gather | bytes 24000 | tf_op jit(solution)/shard_map/all_gather | solution.py:190
  177.3 22.3 %collective-permute-done.1 = bf16[1,128,1600]{1,2,0:T(8,128)(2,1)S(1)} collective-permute-done((bf16[1,128,1600]{1,2,0:T(8,128)(2,1)S(1)}, bf16[1,128,1600]{1,2,0:T(8,128)(2,1)S(1)}, u32[]{:S(2)}, u32[]{:S(2)}) %collective-permute-start.1) | collective-permute-done | bytes 409632 | tf_op jit(solution)/shard_map/ppermute | solution.py:26
  210.9 28.2 %collective-permute-done.2 = bf16[2,128,1600]{1,2,0:T(8,128)(2,1)} collective-permute-done((bf16[2,128,1600]{1,2,0:T(8,128)(2,1)}, bf16[2,128,1600]{1,2,0:T(8,128)(2,1)}, u32[]{:S(2)}, u32[]{:S(2)}) %collective-permute-start.2) | collective-permute-done | bytes 819232 | tf_op jit(solution)/shard_map/ppermute | solution.py:26
  245.7 8.0 %convolution_add_fusion = f32[512,1600]{0,1:T(8,128)} fusion(bf16[512,1600]{1,0:T(8,128)(2,1)} %bitcast.219, bf16[1600,1600]{1,0:T(8,128)(2,1)} %all-gather.15.cloned.1.call-done, f32[1600]{0:T(1024)S(1)} %copy-done.27), kind=kOutput, calls=%fused_computation.16 | convolution fusion | flops 2622259200 | bytes 10041600 | tf_op jit(solution)/shard_map/dot_general | solution.py:50
  256.0 9.4 %fusion.91 = (f32[1600]{0:T(1024)S(1)}, bf16[512,1600]{0,1:T(8,128)(2,1)S(1)}) fusion(f32[512,1600]{0,1:T(8,128)} %convolution_add_fusion, bf16[512,1600]{1,0:T(8,128)(2,1)} %bitcast.217, bf16[1600,1600]{1,0:T(8,128)(2,1)} %all-gather.17.cloned.1.call-done), kind=kOutput, calls=%fused_computation.138 | convolution fusion | flops 2637822464 | bytes 11680000 | tf_op jit(solution)/shard_map/dot_general | solution.py:50
  274.6 8.0 %convolution_convert_fusion.6 = bf16[512,1600]{0,1:T(8,128)(2,1)} fusion(bf16[1600,1600]{1,0:T(8,128)(2,1)} %all-gather.17.cloned.1.call-done, f32[512,1600]{0,1:T(8,128)} %convolution_add_fusion), kind=kOutput, calls=%fused_computation.18 | convolution fusion | flops 2629632000 | bytes 10035200 | tf_op jit(solution)/shard_map/dot_general | solution.py:50
  286.2 7.6 %convolution_convert_fusion.1 = bf16[1600,1600]{1,0:T(8,128)(2,1)} fusion(bf16[512,1600]{1,0:T(8,128)(2,1)} %bitcast.220, bf16[512,1600]{0,1:T(8,128)(2,1)} %copy-done.30), kind=kOutput, calls=%fused_computation.3 | convolution fusion | flops 2624000000 | bytes 8396800 | tf_op jit(solution)/shard_map/dot_general | solution.py:50
  293.9 8.2 %convolution_convert_fusion = bf16[1600,1600]{1,0:T(8,128)(2,1)} fusion(bf16[512,1600]{1,0:T(8,128)(2,1)} %bitcast.218, f32[512,1600]{0,1:T(8,128)} %convolution_add_fusion), kind=kOutput, calls=%fused_computation.2 | convolution fusion | flops 2631372800 | bytes 10035200 | tf_op jit(solution)/shard_map/dot_general | solution.py:50
  310.7 37.4 %reduce-scatter.27.cloned.1.call-done = bf16[128,1600]{1,0:T(8,128)(2,1)} async-done(((bf16[512,1600]{1,0:T(8,128)(2,1)}), bf16[128,1600]{1,0:T(8,128)(2,1)}) %reduce-scatter.27.cloned.1.call-update) | async-done | bytes 409616
  380.9 33.7 %reduce-scatter.37.cloned.1.call-done = bf16[200,1600]{1,0:T(8,128)(2,1)} async-done(((bf16[1600,1600]{1,0:T(8,128)(2,1)}), bf16[200,1600]{1,0:T(8,128)(2,1)}) %reduce-scatter.37.cloned.1.call-update) | async-done | bytes 640016
  418.6 61.7 %reduce-scatter.39.cloned.1.call-done = bf16[200,1600]{1,0:T(8,128)(2,1)} async-done(((bf16[1600,1600]{1,0:T(8,128)(2,1)}), bf16[200,1600]{1,0:T(8,128)(2,1)}) %reduce-scatter.39.cloned.1.call-update) | async-done | bytes 640016
  481.3 59.9 %all-gather.19.cloned.1.call-done = bf16[512,4,1200]{0,2,1:T(8,128)(2,1)} async-done(((bf16[128,4,1200]{0,2,1:T(8,128)(2,1)}), bf16[512,4,1200]{0,2,1:T(8,128)(2,1)}) %all-gather.19.cloned.1.call-update) | async-done | bytes 4915216 | tf_op jit(solution)/shard_map/all_gather | solution.py:77
  541.2 6.1 multiply_reduce_fusion.1
  548.3 58.9 %reduce-scatter.35.cloned.1.call-done = bf16[200,1600]{1,0:T(8,128)(2,1)} async-done(((bf16[1600,1600]{1,0:T(8,128)(2,1)}), bf16[200,1600]{1,0:T(8,128)(2,1)}) %reduce-scatter.35.cloned.1.call-update) | async-done | bytes 640016
  609.5 6.7 convolution_convert_fusion.4
  619.7 10.8 %all-to-all-done.1 = f32[128,4,400]{0,2,1:T(8,128)S(1)} async-done(((f32[128,4,400]{0,2,1:T(8,128)}), f32[128,4,400]{0,2,1:T(8,128)S(1)}, u32[]{:S(2)}, u32[]{:S(2)}) %all-to-all-start.1) | async-done | bytes 819232 | tf_op jit(solution)/shard_map/all_to_all | solution.py:101
  641.0 8.1 %all-reduce.4 = (f32[512,1]{0,1:T(1,128)S(1)}, f32[512,1]{0,1:T(1,128)S(1)}) all-reduce(f32[512,1]{0,1:T(1,128)S(1)} %bitcast.273, f32[512,1]{0,1:T(1,128)S(1)} %bitcast.274), channel_id=1, replica_groups=mesh['dp'=2,'wide'=4,'narrow'=4] {'wide'}, use_global_device_ids=true, to_apply=%region_16.17 | all-reduce | flops 1024 | bytes 8192 | tf_op jit(solution)/shard_map/psum | solution.py:54
  650.3 43.6 %all-reduce.8.cloned.1.call-done = (f32[3,1600]{1,0:T(4,128)}, f32[5,1600]{1,0:T(8,128)}, f32[6400]{0:T(1024)}) async-done(((f32[3,1600]{1,0:T(4,128)}, f32[5,1600]{1,0:T(8,128)}, f32[6400]{0:T(1024)}), (f32[3,1600]{1,0:T(4,128)}, f32[5,1600]{1,0:T(8,128)}, f32[6400]{0:T(1024)})) %all-reduce.8.cloned.1.call-update) | async-done | bytes 76816 | tf_op jit(solution)/shard_map/psum | solution.py:278
  (211 shorter events, 175.2 us)
Async XLA Ops:
  8.0 56.6 %all-gather.11.cloned.1.call-start = ((), (), s32[]{:S(2)}) async-start(), calls=%async_computation.12 | async-start | bytes 4608000 | tf_op jit(solution)/shard_map/all_gather | solution.py:184
  18.0 144.5 %reduce-scatter.25.cloned.1.call-start = ((), (), s32[]{:S(2)}) async-start(), calls=%async_computation.19 | async-start | bytes 6225920
  80.3 91.4 %all-gather.13.cloned.1.call-start = ((), (), s32[]{:S(2)}) async-start(), calls=%async_computation.13 | async-start | bytes 5990400 | tf_op jit(solution)/shard_map/all_gather | solution.py:187
  103.3 142.4 %all-gather.15.cloned.1.call-start = ((), (), s32[]{:S(2)}) async-start(), calls=%async_computation.14 | async-start | bytes 5990400 | tf_op jit(solution)/shard_map/all_gather | solution.py:188
  104.3 151.7 %all-gather.17.cloned.1.call-start = ((), (), s32[]{:S(2)}) async-start(), calls=%async_computation.15 | async-start | bytes 5990400 | tf_op jit(solution)/shard_map/all_gather | solution.py:189
  107.7 23.4 %all-to-all-start.2 = ((f32[4,128,400]{1,2,0:T(8,128)}), f32[4,128,400]{1,2,0:T(8,128)S(1)}, u32[]{:S(2)}, u32[]{:S(2)}) async-start(f32[4,128,400]{1,2,0:T(8,128)} %copy_bitcast_fusion), calls=%async_computation.2 | async-start | bytes 1638400 | tf_op jit(solution)/shard_map/all_to_all | solution.py:97
  111.2 47.1 %collective-permute-start = (s32[1,128]{1,0:T(1,128)S(1)}, s32[1,128]{1,0:T(1,128)S(1)}, u32[]{:S(2)}, u32[]{:S(2)}) collective-permute-start(s32[1,128]{1,0:T(1,128)S(1)} %copy-done.29), channel_id=1, source_target_pairs={{0,0},{4,1},{8,2},{12,3},{1,4},{5,5},{9,6},{13,7},{2,8},{6,9},{10,... | collective-permute-start | bytes 1544 | tf_op jit(solution)/shard_map/ppermute | solution.py:181
  131.1 40.7 %all-to-all-start = ((f32[4,128,400]{1,2,0:T(8,128)}), f32[4,128,400]{1,2,0:T(8,128)}, u32[]{:S(2)}, u32[]{:S(2)}) async-start(f32[4,128,400]{1,2,0:T(8,128)} %copy_bitcast_fusion.1), calls=%async_computation | async-start | bytes 1638400 | tf_op jit(solution)/shard_map/all_to_all | solution.py:97
  135.3 174.2 %reduce-scatter.29.cloned.1.call-start = ((), (), s32[]{:S(2)}) async-start(), calls=%async_computation.21 | async-start | bytes 2129920
  135.4 23.0 %collective-permute-start.3 = (bf16[1,128,1600]{1,2,0:T(8,128)(2,1)S(1)}, bf16[1,128,1600]{1,2,0:T(8,128)(2,1)S(1)}, u32[]{:S(2)}, u32[]{:S(2)}) collective-permute-start(bf16[1,128,1600]{1,2,0:T(8,128)(2,1)S(1)} %bitcast.231), channel_id=1, source_target_pairs={{0,1},{1,0},{2,3},{3,2},{4,5},{5,4},{6,7},{7,6},{8,9},{9,8},{10,11... | collective-permute-start | bytes 1228808 | tf_op jit(solution)/shard_map/ppermute | solution.py:26
  159.9 44.6 %collective-permute-start.4 = (bf16[2,128,1600]{1,2,0:T(8,128)(2,1)}, bf16[2,128,1600]{1,2,0:T(8,128)(2,1)}, u32[]{:S(2)}, u32[]{:S(2)}) collective-permute-start(bf16[2,128,1600]{1,2,0:T(8,128)(2,1)} %get-tuple-element.96), channel_id=1, source_target_pairs={{0,2},{1,3},{2,0},{3,1},{4,6},{5,7},{6,4},{7,5},{8,10},{9,11},{10,... | collective-permute-start | bytes 2457608 | tf_op jit(solution)/shard_map/ppermute | solution.py:26
  176.7 22.8 %collective-permute-start.1 = (bf16[1,128,1600]{1,2,0:T(8,128)(2,1)S(1)}, bf16[1,128,1600]{1,2,0:T(8,128)(2,1)S(1)}, u32[]{:S(2)}, u32[]{:S(2)}) collective-permute-start(bf16[1,128,1600]{1,2,0:T(8,128)(2,1)S(1)} %fusion.125), channel_id=1, source_target_pairs={{0,1},{1,0},{2,3},{3,2},{4,5},{5,4},{6,7},{7,6},{8,9},{9,8},{10,11... | collective-permute-start | bytes 1228808 | tf_op jit(solution)/shard_map/ppermute | solution.py:26
  201.0 38.2 %collective-permute-start.2 = (bf16[2,128,1600]{1,2,0:T(8,128)(2,1)}, bf16[2,128,1600]{1,2,0:T(8,128)(2,1)}, u32[]{:S(2)}, u32[]{:S(2)}) collective-permute-start(bf16[2,128,1600]{1,2,0:T(8,128)(2,1)} %get-tuple-element.98), channel_id=1, source_target_pairs={{0,2},{1,3},{2,0},{3,1},{4,6},{5,7},{6,4},{7,5},{8,10},{9,11},{10,... | collective-permute-start | bytes 2457608 | tf_op jit(solution)/shard_map/ppermute | solution.py:26
  274.3 73.8 %reduce-scatter.27.cloned.1.call-start = ((), (), s32[]{:S(2)}) async-start(), calls=%async_computation.20 | async-start | bytes 2129920
  286.1 128.5 %reduce-scatter.37.cloned.1.call-start = ((), (), s32[]{:S(2)}) async-start(), calls=%async_computation.25 | async-start | bytes 5990400
  293.8 186.5 %reduce-scatter.39.cloned.1.call-start = ((), (), s32[]{:S(2)}) async-start(), calls=%async_computation.26 | async-start | bytes 5990400
  302.1 239.1 %all-gather.19.cloned.1.call-start = ((), (), s32[]{:S(2)}) async-start(), calls=%async_computation.16 | async-start | bytes 6144000 | tf_op jit(solution)/shard_map/all_gather | solution.py:77
  375.7 231.4 %reduce-scatter.35.cloned.1.call-start = ((), (), s32[]{:S(2)}) async-start(), calls=%async_computation.24 | async-start | bytes 5990400
  380.9 254.1 %all-gather.21.cloned.1.call-start = ((), (), s32[]{:S(2)}) async-start(), calls=%async_computation.17 | async-start | bytes 1996800 | tf_op jit(solution)/shard_map/all_gather | solution.py:229
  414.6 223.4 %all-gather.23.cloned.1.call-start = ((), (), s32[]{:S(2)}) async-start(), calls=%async_computation.18 | async-start | bytes 1996800 | tf_op jit(solution)/shard_map/all_gather | solution.py:229
  480.4 213.5 %all-reduce.8.cloned.1.call-start = ((), (), s32[]{:S(2)}) async-start(), calls=%async_computation.27 | async-start | bytes 217088 | tf_op jit(solution)/shard_map/psum | solution.py:278
  548.2 151.4 %reduce-scatter.33.cloned.1.call-start = ((), (), s32[]{:S(2)}) async-start(), calls=%async_computation.23 | async-start | bytes 1024000
  609.4 98.8 %reduce-scatter.31.cloned.1.call-start = ((), (), s32[]{:S(2)}) async-start(), calls=%async_computation.22 | async-start | bytes 4608000 | tf_op jit(solution)/shard_map/reduce_scatter | solution.py:249
  630.5 18.6 %all-to-all-start.3 = ((f32[128,4,400]{0,2,1:T(8,128)}), f32[128,4,400]{0,2,1:T(8,128)S(1)}, u32[]{:S(2)}, u32[]{:S(2)}) async-start(f32[128,4,400]{0,2,1:T(8,128)} %bitcast.51), calls=%async_computation.3 | async-start | bytes 1638400 | tf_op jit(solution)/shard_map/all_to_all | solution.py:101
  (32 other events, 515.8 us)
Sparse Core Ops, SparseCore 0:
  18.1 46.4 all-gather.10
  80.5 74.4 reduce-scatter.24
  274.4 35.0 reduce-scatter.28
  311.7 36.3 reduce-scatter.26
  351.3 63.2 reduce-scatter.36
  417.9 62.4 reduce-scatter.38
  482.7 58.4 all-gather.18
  544.6 62.4 reduce-scatter.34
  608.7 10.4 all-gather.20
  620.6 10.6 all-gather.22
  634.1 21.9 reduce-scatter.32
  658.3 49.9 reduce-scatter.30
Sparse Core Ops, SparseCore 1:
  103.4 66.6 all-gather.12
  171.8 41.2 all-gather.14
  214.8 41.2 all-gather.16
  548.3 145.5 all-reduce.7
